TPU v7x, 32 devices: a whole 2x2x4 slice. The times are simulated.
32 devices in a mesh: dp: 2 (over x), ep: 16 (over y, z, core).
Axes of the slice: x: 2, y: 2, z: 4, core: 2. Of those that a mesh axis runs over, the one named last changes fastest.
Arguments:
- x: bfloat16 [2, 16, 256, 2560], P('dp', 'ep'), parts along dimension 0
- expert: int32 [2, 16, 256, 1], P('dp', 'ep'), parts along dimension 0
- slot: int32 [2, 16, 256, 1], P('dp', 'ep'), parts along dimension 0
- gate: float32 [2, 16, 256, 1], P('dp', 'ep'), parts along dimension 0
- w_gate: bfloat16 [16, 2560, 8192], P('ep')
- w_up: bfloat16 [16, 2560, 8192], P('ep')
- w_down: bfloat16 [16, 8192, 2560], P('ep')
- s_gate: bfloat16 [2560, 8192], replicated
- s_up: bfloat16 [2560, 8192], replicated
- s_down: bfloat16 [8192, 2560], replicated
Outputs:
- y: bfloat16 [2, 16, 256, 2560], P('dp', 'ep'), parts along dimension 0
There are 2 independent parts. A program takes and returns all parts, laid end to end along the dimension named above; an argument that names none is the same for every part.
All inputs are finite; a program needn't handle non-finite values.
Results may differ from a plain program's by a relative error of at most 0.009.
Values are sent between devices in bfloat16 or wider.
A program may use at most 2 GiB of HBM per device.

v0:
```python
import jax
import jax.numpy as jnp
from jax import lax
from jax.sharding import NamedSharding, PartitionSpec as P


def einsum(form, a, b):
    return jnp.einsum(form, a.astype(jnp.float32), b.astype(jnp.float32))


def for_all(x, s_gate, s_up, s_down):
    h = jax.nn.silu(einsum("...d,df->...f", x, s_gate)) * einsum("...d,df->...f", x, s_up)
    return einsum("...f,fd->...d", h.astype(jnp.bfloat16), s_down)


def solution(mesh):
    def placed(v, *spec):
        return lax.with_sharding_constraint(v, NamedSharding(mesh, P(*spec)))

    def step(x, expert, slot, gate, w_gate, w_up, w_down, s_gate, s_up, s_down):
        experts, (tokens, top) = w_gate.shape[0], expert.shape[2:]
        slots = 5 * tokens * top // (4 * experts)
        to_expert = jax.nn.one_hot(expert, experts, dtype=jnp.bfloat16)
        to_slot = jax.nn.one_hot(slot, slots, dtype=jnp.bfloat16)
        weighted = to_expert * gate[..., None].astype(jnp.bfloat16)
        dispatch = einsum("abtke,abtkc->abtec", to_expert, to_slot).astype(jnp.bfloat16)
        combine = einsum("abtke,abtkc->abtec", weighted, to_slot).astype(jnp.bfloat16)
        z = einsum("abtec,abtd->aebcd", dispatch, x).astype(jnp.bfloat16)
        z = placed(z, "dp", None, "ep", None, None)
        z = placed(z, "dp", "ep", None, None, None)
        h = jax.nn.silu(einsum("aebcd,edf->aebcf", z, w_gate))
        h = (h * einsum("aebcd,edf->aebcf", z, w_up)).astype(jnp.bfloat16)
        out = einsum("aebcf,efd->aebcd", h, w_down).astype(jnp.bfloat16)
        out = placed(out, "dp", "ep", None, None, None)
        out = placed(out, "dp", None, "ep", None, None)
        y = einsum("abtec,aebcd->abtd", combine, out)
        return (y + for_all(x, s_gate, s_up, s_down)).astype(jnp.bfloat16)

    return step
```

profile of v0, /device:TPU:0, one launch (start us, length us, event | category | flops | bytes accessed | tf_op | source)
XLA Modules:
  0.0 185.7 jit_solution(2357196795130465410)
XLA Ops:
  0.0 0.0 copy-start
  0.0 0.8 convert_bitcast_fusion
  0.8 0.0 copy-start.1
  0.8 0.7 convert_bitcast_fusion.1
  1.5 0.0 copy-done.1
  1.5 0.0 copy-done
  1.5 2.0 %fusion.27 = bf16[1,16,1,1,20,2560]{5,4,3,2,0,1:T(8,128)(2,1)} fusion(bf16[1,1,256,2560]{3,2,1,0:T(8,128)(2,1)S(1)} %copy-done, f32[256,16]{0,1:T(8,128)S(1)} %convert_bitcast_fusion.1, f32[256,20]{0,1:T(8,128)S(1)} %convert_bitcast_fusion), kind=kOutput, calls=%fused_computation.24 | convolution fusion | flops 420413440 | bytes 2985984 | tf_op jit(solution)/abtec,abtd->aebcd/dot_general | solution.py:8
  3.5 7.4 %all-to-all-start = ((bf16[1,16,1,1,20,2560]{5,4,3,2,0,1:T(8,128)(2,1)}), bf16[1,16,1,1,20,2560]{5,4,3,2,0,1:T(8,128)(2,1)S(1)}, u32[]{:S(2)}, u32[]{:S(2)}) async-start(bf16[1,16,1,1,20,2560]{5,4,3,2,0,1:T(8,128)(2,1)} %fusion.27), calls=%async_computation | async-start | bytes 3932160 | tf_op jit(solution)/sharding_constraint;jit(solution)/sharding_constraint | solution.py:18
  10.9 0.7 convert_reduce_fusion
  11.6 1.3 fusion.52
  12.9 20.6 %convolution_bitcast_fusion.1 = f32[1,1,256,8192]{3,2,1,0:T(8,128)} fusion(bf16[2560,8192]{1,0:T(8,128)(2,1)} %param.7, bf16[1,1,256,2560]{3,2,1,0:T(8,128)(2,1)S(1)} %copy-done), kind=kOutput, calls=%fused_computation.15 | convolution fusion | flops 10737418240 | bytes 51642368 | tf_op jit(solution)/...d,df->...f/dot_general | solution.py:8
  33.5 20.9 %all-to-all-done = bf16[1,16,1,1,20,2560]{5,4,3,2,0,1:T(8,128)(2,1)S(1)} async-done(((bf16[1,16,1,1,20,2560]{5,4,3,2,0,1:T(8,128)(2,1)}), bf16[1,16,1,1,20,2560]{5,4,3,2,0,1:T(8,128)(2,1)S(1)}, u32[]{:S(2)}, u32[]{:S(2)}) %all-to-all-start) | async-done | bytes 1638432 | tf_op jit(solution)/sharding_constraint;jit(solution)/sharding_constraint | solution.py:18
  54.4 26.2 %fusion.4 = f32[16,20,8192]{2,1,0:T(8,128)} fusion(bf16[1,2560,8192]{2,1,0:T(8,128)(2,1)} %param.4, bf16[1,16,1,1,20,2560]{5,4,3,2,0,1:T(8,128)(2,1)S(1)} %all-to-all-done), kind=kOutput, calls=%fused_computation.4 | convolution fusion | flops 13421772800 | bytes 54067200 | tf_op jit(solution)/aebcd,edf->aebcf/dot_general | solution.py:8
  80.6 26.0 %fusion.14.clone.8 = bf16[16,20,8192]{2,1,0:T(8,128)(2,1)} fusion(bf16[1,2560,8192]{2,1,0:T(8,128)(2,1)} %param.5, f32[16,20,8192]{2,1,0:T(8,128)} %fusion.4, bf16[1,16,1,1,20,2560]{5,4,3,2,0,1:T(8,128)(2,1)S(1)} %all-to-all-done), kind=kOutput, calls=%fused_computation.17.clone.clone.clone.clone.clone.clone.clone.1 | convolution fusion | flops 13437501440 | bytes 59310080 | tf_op jit(solution)/aebcd,edf->aebcf/dot_general | solution.py:8
  106.6 26.5 %fusion.29 = bf16[1,1,16,1,20,2560]{5,4,3,1,0,2:T(8,128)(2,1)} fusion(bf16[1,8192,2560]{2,1,0:T(8,128)(2,1)} %param.6, bf16[16,20,8192]{2,1,0:T(8,128)(2,1)} %fusion.14.clone.8), kind=kOutput, calls=%fused_computation.26 | convolution fusion | flops 13422592000 | bytes 48824320 | tf_op jit(solution)/aebcf,efd->aebcd/dot_general | solution.py:8
  133.1 5.4 %all-to-all-start.1 = ((bf16[1,1,16,1,20,2560]{5,4,3,1,0,2:T(8,128)(2,1)}), bf16[1,1,16,1,20,2560]{5,4,3,1,0,2:T(8,128)(2,1)S(1)}, u32[]{:S(2)}, u32[]{:S(2)}) async-start(bf16[1,1,16,1,20,2560]{5,4,3,1,0,2:T(8,128)(2,1)} %fusion.29), calls=%async_computation.1 | async-start | bytes 3932160 | tf_op jit(solution)/sharding_constraint;jit(solution)/sharding_constraint | solution.py:18
  138.5 0.0 copy-start.2
  138.5 0.0 copy-start.3
  138.5 35.1 %fusion.54 = f32[256,2560]{1,0:T(8,128)} fusion(bf16[8192,2560]{1,0:T(8,128)(2,1)} %param.9, bf16[2560,8192]{1,0:T(8,128)(2,1)} %param.8, f32[1,1,256,8192]{3,2,1,0:T(8,128)} %convolution_bitcast_fusion.1, bf16[1,1,256,2560]{3,2,1,0:T(8,128)(2,1)S(1)} %copy-done), kind=kOutput, calls=%fused_computation.51 | convolution fusion | flops 21487419392 | bytes 96206848 | tf_op jit(solution)/...f,fd->...d/dot_general | solution.py:8
  173.7 8.3 %all-to-all-done.1 = bf16[1,1,16,1,20,2560]{5,4,3,1,0,2:T(8,128)(2,1)S(1)} async-done(((bf16[1,1,16,1,20,2560]{5,4,3,1,0,2:T(8,128)(2,1)}), bf16[1,1,16,1,20,2560]{5,4,3,1,0,2:T(8,128)(2,1)S(1)}, u32[]{:S(2)}, u32[]{:S(2)}) %all-to-all-start.1) | async-done | bytes 1638432 | tf_op jit(solution)/sharding_constraint;jit(solution)/sharding_constraint | solution.py:18
  182.0 0.0 copy-done.2
  182.0 0.0 copy-done.3
  182.0 3.7 %fusion.34 = bf16[1,1,256,2560]{3,2,1,0:T(8,128)(2,1)} fusion(f32[256,2560]{1,0:T(8,128)} %fusion.54, bf16[1,1,16,1,20,2560]{5,4,3,1,0,2:T(8,128)(2,1)S(1)} %all-to-all-done.1, f32[256,20]{0,1:T(8,128)S(1)} %copy-done.2, f32[256,16]{0,1:T(8,128)S(1)} %copy-done.3), kind=kOutput, calls=%fused_computation.27 | convolution fusion | flops 420904960 | bytes 5607424 | tf_op jit(solution)/abtec,aebcd->abtd/dot_general | solution.py:8
Async XLA Ops:
  0.0 1.5 copy-start
  0.8 0.7 copy-start.1
  3.5 50.9 %all-to-all-start = ((bf16[1,16,1,1,20,2560]{5,4,3,2,0,1:T(8,128)(2,1)}), bf16[1,16,1,1,20,2560]{5,4,3,2,0,1:T(8,128)(2,1)S(1)}, u32[]{:S(2)}, u32[]{:S(2)}) async-start(bf16[1,16,1,1,20,2560]{5,4,3,2,0,1:T(8,128)(2,1)} %fusion.27), calls=%async_computation | async-start | bytes 3932160 | tf_op jit(solution)/sharding_constraint;jit(solution)/sharding_constraint | solution.py:18
  133.1 48.9 %all-to-all-start.1 = ((bf16[1,1,16,1,20,2560]{5,4,3,1,0,2:T(8,128)(2,1)}), bf16[1,1,16,1,20,2560]{5,4,3,1,0,2:T(8,128)(2,1)S(1)}, u32[]{:S(2)}, u32[]{:S(2)}) async-start(bf16[1,1,16,1,20,2560]{5,4,3,1,0,2:T(8,128)(2,1)} %fusion.29), calls=%async_computation.1 | async-start | bytes 3932160 | tf_op jit(solution)/sharding_constraint;jit(solution)/sharding_constraint | solution.py:18
  138.5 43.5 %copy-start.2 = (f32[256,20]{0,1:T(8,128)S(1)}, f32[256,20]{0,1:T(8,128)}, u32[]{:S(2)}) copy-start(f32[256,20]{0,1:T(8,128)} %copy-done.1) | copy-start | bytes 61444
  138.5 43.5 %copy-start.3 = (f32[256,16]{0,1:T(8,128)S(1)}, f32[256,16]{0,1:T(8,128)}, u32[]{:S(2)}) copy-start(f32[256,16]{0,1:T(8,128)} %fusion.52) | copy-start | bytes 49156
where the time goes:
time: 187 us; the launch traced here: 186 us
  matrix products  140 us (75%)
  waiting for transfers between devices  29.3 us (16%)
  starting transfers between devices  12.8 us (7%)
  other arithmetic  3.47 us (2%)
    dot_general x7, matrix products, einsum(): return jnp.einsum(form, a.astype(jnp.float32), b.astype(jnp.float32))  140 us
    another operation x2, waiting for transfers between devices, placed(): return lax.with_sharding_constraint(v, NamedSharding(mesh, P(*spec)))  29.3 us
    another operation x2, starting transfers between devices, placed(): return lax.with_sharding_constraint(v, NamedSharding(mesh, P(*spec)))  12.8 us
  transfers between devices with their start and end apart: 2, of which 2 were waited for; matrix products, arithmetic and copies ran while one was open for 31% of the time, Pallas kernels for 0%

commit v1 on v0

v1 whole, which is shorter than its diff:
```python
import functools

import jax
import jax.numpy as jnp
from jax import lax
from jax.experimental import pallas as pl
from jax.experimental.pallas import tpu as pltpu
from jax.sharding import PartitionSpec as P

MESH = pl.DeviceIdType.MESH
CH = 512
RT = 4
FIRST, EXTRA = 16, 4
LANES = 128
BUFS = 8
PLAN = ((6, 5),)


def mm(a, b):
    return jnp.dot(a, b, preferred_element_type=jnp.float32)


def silu(g):
    return g * jax.nn.sigmoid(g)


def at_col(c, width=CH):
    return pl.ds(c * width if isinstance(c, int) else pl.multiple_of(c * width, width), width)


class Schedule:
    def __init__(self, bufs):
        self.bufs, self.stages = bufs, []

    def add(self, count, *steps):
        self.stages.append((count, steps))
        return len(self.stages) - 1

    def finish(self):
        self.tiles, self.first, at = [], {}, 0
        for s, (count, steps) in enumerate(self.stages):
            for turn in range(count):
                for p, step in enumerate(steps):
                    self.first[s, turn, p] = len(self.tiles)
                    for q, (kind, start, per) in enumerate(step):
                        self.tiles.append((kind, start + per * turn, (s, p, q), turn))
        self.reads, issued = {}, min(self.bufs, len(self.tiles))
        for s, (count, steps) in enumerate(self.stages):
            for turn in range(count):
                for p in range(len(steps)):
                    upto = min(self.first[s, turn, p] + self.bufs, len(self.tiles))
                    self.reads[s, turn, p] = list(range(issued, max(issued, upto)))
                    issued = max(issued, upto)
        assert issued == len(self.tiles)

    def groups(self, s, p):
        found = {}
        for turn in range(self.stages[s][0]):
            for m, n in enumerate(self.reads[s, turn, p]):
                kind, index, where, _ = self.tiles[n]
                found.setdefault((where, m), []).append((turn, kind, index, n))
        out = []
        for entries in found.values():
            while entries:
                run = entries[:2]
                if len(run) == 2:
                    d = [run[1][i] - run[0][i] for i in (0, 2, 3)]
                    for e in entries[2:]:
                        if [e[i] - run[-1][i] for i in (0, 2, 3)] != d:
                            break
                        run.append(e)
                    slope = (d[1] // d[0], d[2] // d[0])
                    assert slope[0] * d[0] == d[1] and slope[1] * d[0] == d[2]
                    gap = d[0]
                else:
                    slope, gap = (0, 0), 1
                t0, kind, i0, n0 = run[0]
                out.append((t0, run[-1][0], gap, kind, (i0, slope[0]), (n0, slope[1])))
                entries = entries[len(run):]
        return out


def kernel(
    plan,
    x_hbm, expert_ref, slot_ref, gate_ref, wg, wu, wd, sg, su, sd, y_hbm,
    ring, x_ref, gates, ups, h_ref, z_out, z_in, r_out, r_in, total, gs, us, hs, acc, zk, send_to, take, fold, unfold, y_ref,
    ring_sem, x_sem, y_sem, z_out_sem, z_in_sem, r_out_sem, r_in_sem,
):
    members, tokens = z_out.shape[1], x_ref.shape[0]
    D, F = x_ref.shape[1], h_ref.shape[1]
    chunks, blocks = D // CH, F // CH
    tile_rows = RT * CH
    groups = F // tile_rows
    me, group = lax.axis_index("ep"), lax.axis_index("dp")

    def peer(d):
        at = me
        for i in range(4):
            if d >> i & 1:
                at = at + (1 << i) * (1 - 2 * ((me // (1 << i)) % 2))
        return (group, at)

    def copies(kind, i, slot):
        if kind in ("sg", "su"):
            w = sg if kind == "sg" else su
            return [(w.at[:, at_col(i)], ring.at[slot, pl.ds(0, D)])]
        if kind == "sd":
            rows = at_col(i)
            return [(sd.at[rows, at_col(c)], ring.at[slot, at_col(c)]) for c in range(chunks)]
        if kind in ("wg", "wu"):
            w = wg if kind == "wg" else wu
            k, b = i // groups, i % groups
            return [(w.at[0, at_col(k), at_col(b * RT + j)], ring.at[slot, at_col(j)]) for j in range(RT)]
        c, b = i // groups, i % groups
        return [(wd.at[0, at_col(b, tile_rows), at_col(c)], ring.at[slot, pl.ds(0, tile_rows)])]

    def read(kind, i, slot):
        for src, dst in copies(kind, i, slot):
            pltpu.make_async_copy(src, dst, ring_sem.at[slot]).start()

    def landed(kind, slot):
        rows = D if kind[0] == "s" else tile_rows
        block = ring.at[slot, pl.ds(0, rows)]
        pltpu.make_async_copy(block, block, ring_sem.at[slot]).wait()

    sched = Schedule(BUFS)

    def enter(s, p, turn):
        count, steps = sched.stages[s]
        for t0, t1, gap, kind, (i0, di), (n0, dn) in sched.groups(s, p):
            def go(kind=kind, t0=t0, i0=i0, di=di, n0=n0, dn=dn):
                past = turn - t0
                read(kind, i0 + di * past, (n0 + dn * past) % BUFS)

            if isinstance(turn, int):
                if t0 <= turn <= t1 and (turn - t0) % gap == 0:
                    go()
            elif t0 == 0 and t1 == count - 1 and gap == 1:
                go()
            else:
                here = jnp.logical_and(turn >= t0, turn <= t1)
                if gap > 1:
                    here = jnp.logical_and(here, (turn - t0 + gap * count) % gap == 0)
                pl.when(here)(go)
        per = sum(len(step) for step in steps)
        slots = [(sched.first[s, 0, p] + per * turn + q) % BUFS for q in range(len(steps[p]))]
        for slot, (kind, _, _) in zip(slots, steps[p]):
            landed(kind, slot)
        return slots

    def run(s, body):
        count = sched.stages[s][0]
        if count == 1:
            body(0)
        elif count > 1:
            lax.fori_loop(0, count, lambda t, c: (body(t), c)[1], 0)

    def shared_up(g_slot, u_slot):
        gs[...] = mm(x_ref[...], ring[g_slot, pl.ds(0, D), :])
        us[...] = mm(x_ref[...], ring[u_slot, pl.ds(0, D), :])

    def shared_h():
        hs[...] = (silu(gs[...]) * us[...]).astype(hs.dtype)

    def shared_down(slot):
        for c in range(chunks):
            total[:, at_col(c)] += mm(hs[...], ring[slot, at_col(c), :])

    def pack(z, out, own, c):
        main = members * FIRST
        out[c, :, :, pl.ds(0, CH)] = z[:main].reshape(members, FIRST, CH)
        rest = jnp.concatenate([z[main:, g * LANES:(g + 1) * LANES] for g in range(CH // LANES)], axis=0)
        rest = mm(fold[...], rest).astype(z.dtype).reshape(members, FIRST, LANES)
        out[c, :, :, pl.ds(CH, LANES)] = rest
        own[c, 0, :, pl.ds(0, CH)] = z[:FIRST]
        own[c, 0, :, pl.ds(CH, LANES)] = rest[0]

    def unpack(box, c):
        main, extra = members * FIRST, members * EXTRA
        zk[pl.ds(0, main), :] = box[c, :, :, pl.ds(0, CH)].reshape(main, CH)
        rest = mm(unfold[...], box[c, :, :, pl.ds(CH, LANES)].reshape(main, LANES)).astype(zk.dtype)
        for g in range(CH // LANES):
            zk[pl.ds(main, extra), pl.ds(g * LANES, LANES)] = rest[g * extra:(g + 1) * extra]

    far_first = sorted(range(1, members), key=lambda d: (0 if d & 4 else 1, -bin(d & 10).count("1"), d))

    def send(out, box, out_sem, in_sem, c):
        for d in far_first:
            pltpu.make_async_remote_copy(
                src_ref=out.at[c, d], dst_ref=box.at[c, d], send_sem=out_sem.at[c], recv_sem=in_sem.at[c],
                device_id=peer(d), device_id_type=MESH,
            ).start()

    def all_of(box, sem, c):
        others = box.at[c, pl.ds(1, members - 1)]
        pltpu.make_async_copy(others, others, sem.at[c]).wait()

    def routed_up(g_slot, u_slot, b):
        for j in range(RT):
            cols = pl.ds(pl.multiple_of(b * tile_rows + j * CH, CH), CH)
            gates[:, cols] += mm(zk[...], ring[g_slot, at_col(j), :])
            ups[:, cols] += mm(zk[...], ring[u_slot, at_col(j), :])

    def routed_h(b):
        for j in range(RT):
            cols = pl.ds(b * tile_rows + j * CH if isinstance(b, int) else pl.multiple_of(b * tile_rows + j * CH, CH), CH)
            h_ref[:, cols] = (silu(gates[:, cols]) * ups[:, cols]).astype(h_ref.dtype)

    stages, block, chunk = [], 0, 0
    for n_shared, n_chunks in plan:
        if n_shared and block == 0:
            stages.append(("first", sched.add(1, [("sg", 0, 0), ("su", 0, 0)]), 0))
            block, n_shared = 1, n_shared - 1
        if n_shared:
            step = [("sg", block, 1), ("su", block, 1), ("sd", block - 1, 1)]
            stages.append(("shared", sched.add(n_shared, step), 0))
            block += n_shared
        plain = min(n_chunks, chunks - 1 - chunk)
        if plain > 0:
            i0 = chunk * groups
            stages.append(("up", sched.add(plain * groups, [("wg", i0, 1), ("wu", i0, 1)]), chunk))
            chunk, n_chunks = chunk + plain, n_chunks - plain
        if n_chunks > 0 and chunk == chunks - 1:
            i0 = chunk * groups
            stages.append(("last", sched.add(groups, [("wg", i0, 1), ("wu", i0, 1)]), chunk))
            chunk += 1
    assert chunk == chunks and block > 0
    halves = groups // 2
    down0 = [[("wd", 2 * p, 0), ("wd", 2 * p + 1, 0)] for p in range(halves)]
    stages.append(("down0", sched.add(1, *down0), 0))
    down = [[("wd", groups + 2 * p, groups), ("wd", groups + 2 * p + 1, groups)] for p in range(halves)]
    stages.append(("down", sched.add(chunks - 1, *down), 1))
    if block < blocks:
        step = [("sg", block, 1), ("su", block, 1), ("sd", block - 1, 1)]
        stages.append(("shared", sched.add(blocks - block, step), 0))
    stages.append(("end", sched.add(1, [("sd", blocks - 1, 0)]), 0))
    sched.finish()

    x_copy = pltpu.make_async_copy(x_hbm.at[0, 0], x_ref, x_sem)
    x_copy.start()
    for n in range(min(BUFS, len(sched.tiles))):
        kind, i, _, _ = sched.tiles[n]
        read(kind, i, n % BUFS)
    barrier = pltpu.get_barrier_semaphore()
    for d in range(1, members):
        pl.semaphore_signal(barrier, inc=1, device_id=peer(d), device_id_type=MESH)

    slots = members * (FIRST + EXTRA)
    main = members * FIRST
    toward = jnp.bitwise_xor(expert_ref[...], me)
    s = slot_ref[...]
    place = jnp.where(s < FIRST, toward * FIRST + s, main + toward * EXTRA + (s - FIRST))
    place = jnp.where(s < FIRST + EXTRA, place, -1)
    weight = gate_ref[...].astype(jnp.bfloat16).astype(jnp.float32)
    square = lax.broadcasted_iota(jnp.int32, (tokens, tokens), 0) == lax.broadcasted_iota(jnp.int32, (tokens, tokens), 1)

    def upright(row):
        return jnp.sum(jnp.where(square, row, jnp.zeros_like(row)), axis=1, keepdims=True)

    rows = lax.broadcasted_iota(jnp.int32, (slots, tokens), 0)
    send_to[...] = jnp.where(rows == place, 1.0, 0.0).astype(send_to.dtype)
    columns = lax.broadcasted_iota(jnp.int32, (tokens, slots), 1)
    take[...] = jnp.where(columns == upright(place), upright(weight), 0.0).astype(take.dtype)
    r = lax.broadcasted_iota(jnp.int32, (main, main), 0)
    q = lax.broadcasted_iota(jnp.int32, (main, main), 1)

    def folded(r, q):
        extra = members * EXTRA
        return (r // EXTRA) % (FIRST // EXTRA) * extra + r // FIRST * EXTRA + r % EXTRA == q

    fold[...] = jnp.where(folded(r, q), 1.0, 0.0).astype(fold.dtype)
    unfold[...] = jnp.where(folded(q, r), 1.0, 0.0).astype(unfold.dtype)

    x_copy.wait()

    def dispatch(c, carry):
        z = mm(send_to[...], x_ref[:, at_col(c)]).astype(z_out.dtype)
        pack(z, z_out, z_in, c)
        return carry

    lax.fori_loop(0, chunks, dispatch, 0)
    pl.semaphore_wait(barrier, members - 1)

    def ship(c, carry):
        send(z_out, z_in, z_out_sem, z_in_sem, c)
        return carry

    lax.fori_loop(0, chunks, ship, 0)

    def clear(c, carry):
        gates[:, at_col(c)] = jnp.zeros((slots, CH), jnp.float32)
        ups[:, at_col(c)] = jnp.zeros((slots, CH), jnp.float32)
        return carry

    lax.fori_loop(0, blocks, clear, 0)
    total[...] = jnp.zeros_like(total)

    def chunk_here(k):
        all_of(z_in, z_in_sem, k)
        unpack(z_in, k)

    def down_steps(stage, turn, c, first):
        for p in range(halves):
            a, b = enter(stage, p, turn)
            if first and p == 0:
                routed_h(groups - 1)
            part = mm(h_ref[:, pl.ds(2 * p * tile_rows, tile_rows)], ring[a, pl.ds(0, tile_rows), :])
            part += mm(h_ref[:, pl.ds((2 * p + 1) * tile_rows, tile_rows)], ring[b, pl.ds(0, tile_rows), :])
            if p > 0:
                part += acc[...]
            if p < halves - 1:
                acc[...] = part
        pack(part.astype(r_out.dtype), r_out, r_in, c)
        send(r_out, r_in, r_out_sem, r_in_sem, c)

    for name, stage, at in stages:
        if name == "first":
            def body(turn, stage=stage):
                shared_up(*enter(stage, 0, turn))
        elif name == "shared":
            def body(turn, stage=stage):
                g, u, d = enter(stage, 0, turn)
                shared_h()
                shared_up(g, u)
                shared_down(d)
        elif name == "up":
            def body(turn, stage=stage, at=at):
                @pl.when(turn % groups == 0)
                def _():
                    chunk_here(at + turn // groups)

                g, u = enter(stage, 0, turn)
                routed_up(g, u, turn % groups)
        elif name == "last":
            chunk_here(at)

            def body(turn, stage=stage):
                g, u = enter(stage, 0, turn)
                routed_h(jnp.maximum(turn - 1, 0))
                routed_up(g, u, turn)
        elif name == "down0":
            def body(turn, stage=stage):
                down_steps(stage, turn, 0, True)
        elif name == "down":
            def body(turn, stage=stage):
                down_steps(stage, turn, turn + 1, False)
        else:
            def body(turn, stage=stage):
                (d,) = enter(stage, 0, turn)
                shared_h()
                shared_down(d)
        run(stage, body)

    def combine(c, carry):
        all_of(r_in, r_in_sem, c)
        unpack(r_in, c)
        y_ref[:, at_col(c)] = (mm(take[...], zk[...]) + total[:, at_col(c)]).astype(y_ref.dtype)
        pltpu.make_async_copy(y_ref.at[:, at_col(c)], y_hbm.at[0, 0, :, at_col(c)], y_sem.at[c]).start()
        return carry

    lax.fori_loop(0, chunks, combine, 0)

    def settle(c, carry):
        all_of(z_out, z_out_sem, c)
        all_of(r_out, r_out_sem, c)
        pltpu.make_async_copy(y_ref.at[:, at_col(c)], y_hbm.at[0, 0, :, at_col(c)], y_sem.at[c]).wait()
        return carry

    lax.fori_loop(0, chunks, settle, 0)


def solution(mesh):
    def step(x, expert, slot, gate, w_gate, w_up, w_down, s_gate, s_up, s_down):
        _, _, tokens, D = x.shape
        F = w_gate.shape[2]
        members = mesh.shape["ep"]
        chunks, slots = D // CH, members * (FIRST + EXTRA)
        bf16, f32 = jnp.bfloat16, jnp.float32
        plan = PLAN
        box = pltpu.VMEM((chunks, members, FIRST, CH + LANES), bf16)
        sems = pltpu.SemaphoreType.DMA((chunks,))
        hbm = pl.BlockSpec(memory_space=pl.ANY)
        vmem = pl.BlockSpec(memory_space=pltpu.VMEM)
        return pl.pallas_call(
            functools.partial(kernel, plan),
            out_shape=jax.ShapeDtypeStruct(x.shape, x.dtype),
            in_specs=[hbm] + [vmem] * 3 + [hbm] * 6,
            out_specs=hbm,
            scratch_shapes=[
                pltpu.VMEM((BUFS, max(D, RT * CH), CH), bf16),
                pltpu.VMEM((tokens, D), bf16),
                pltpu.VMEM((slots, F), f32),
                pltpu.VMEM((slots, F), f32),
                pltpu.VMEM((slots, F), bf16),
                box, box, box, box,
                pltpu.VMEM((tokens, D), f32),
                pltpu.VMEM((tokens, CH), f32),
                pltpu.VMEM((tokens, CH), f32),
                pltpu.VMEM((tokens, CH), bf16),
                pltpu.VMEM((slots, CH), f32),
                pltpu.VMEM((slots, CH), bf16),
                pltpu.VMEM((slots, tokens), bf16),
                pltpu.VMEM((tokens, slots), bf16),
                pltpu.VMEM((members * FIRST, members * FIRST), bf16),
                pltpu.VMEM((members * FIRST, members * FIRST), bf16),
                pltpu.VMEM((tokens, D), bf16),
                pltpu.SemaphoreType.DMA((BUFS,)),
                pltpu.SemaphoreType.DMA,
                sems, sems, sems, sems, sems,
            ],
            compiler_params=pltpu.CompilerParams(
                collective_id=0, has_side_effects=True, vmem_limit_bytes=67_043_328
            ),
        )(
            x, expert.reshape(1, tokens), slot.reshape(1, tokens), gate.reshape(1, tokens),
            w_gate, w_up, w_down, s_gate, s_up, s_down,
        )

    tok, exp, rep = P("dp", "ep", None, None), P("ep", None, None), P(None, None)
    return jax.shard_map(
        step, mesh=mesh, in_specs=(tok,) * 4 + (exp,) * 3 + (rep,) * 3, out_specs=tok, check_vma=False,
    )
```

time: 187 us -> 112 us (0.60)
  matrix products: 140 us -> 0 us
  Pallas kernels: 0 us -> 109 us
  waiting for transfers between devices: 29.3 us -> 0 us
  starting transfers between devices: 12.8 us -> 0 us
  other arithmetic: 3.47 us -> 0 us
  local copies, waits for them, and re-layouts: 0.02 us -> 2.46 us
    dot_general x7 -> x0, matrix products: 140 us -> none  [einsum(): return jnp.einsum(form, a.astype(jnp.float32), b.astype(jnp.float32))]
    pallas_call x0 -> x1, Pallas kernels: none -> 109 us  [step(): pl.pallas_call(functools.partial(kernel, plan), out_shape=jax.ShapeDtypeS...]
    another operation x2 -> x0, waiting for transfers between devices: 29.3 us -> none  [placed(): return lax.with_sharding_constraint(v, NamedSharding(mesh, P(*spec)))]
    another operation x2 -> x0, starting transfers between devices: 12.8 us -> none  [placed(): return lax.with_sharding_constraint(v, NamedSharding(mesh, P(*spec)))]
    unnamed x3 -> x0, other arithmetic: 2.77 us -> none
    unnamed x8 -> x1, local copies, waits for them, and re-layouts: 0.02 us -> 2.46 us
  transfers between devices with their start and end apart: 2 -> 0, of which waited for: 2 -> 0; matrix products, arithmetic and copies ran while one was open for 31% -> 0% of each run, Pallas kernels for 0% -> 0%
where the time goes in v1:
time: 112 us
  Pallas kernels  109 us (97%)
  local copies, waits for them, and re-layouts  2.46 us (2%)
    pallas_call x1, Pallas kernels, step(): pl.pallas_call(functools.partial(kernel, plan), out_shape=jax.ShapeDtypeS...  109 us
    unnamed x1, local copies, waits for them, and re-layouts  2.46 us

profile of v1, /device:TPU:0, one launch (start us, length us, event | category | flops | bytes accessed | tf_op | source)
XLA Modules:
  0.0 111.7 jit_solution(8584184413483691270)
XLA Ops:
  0.0 109.2 %shard_map.100 = bf16[1,1,256,2560]{3,2,1,0:T(8,128)(2,1)} custom-call(bf16[1,1,256,2560]{3,2,1,0:T(8,128)(2,1)} %x_hbm.1, s32[1,256]{1,0:T(1,128)} %bitcast.3, s32[1,256]{1,0:T(1,128)} %bitcast.4, f32[1,256]{1,0:T(1,128)} %bitcast.5, bf16[1,2560,8192]{2,1,0:T(8,128)(2,1)} %wg.1, bf16[1,2560,8192]{2,1,0:T(8,128)(2,1)} %wu.1, bf16[1,8192,2560]{2,1,0:T(8,128)(2,1)} %wd.1, ...), custom_call_target="tpu_custom_call" | custom-call | tf_op jit(solution)/shard_map/pallas_call | solution.py:384
  109.2 2.5 %copy.12 = bf16[1,1,256,2560]{3,2,1,0:T(8,128)(2,1)} copy(bf16[1,1,256,2560]{3,2,1,0:T(8,128)(2,1)} %shard_map.100) | data formatting | bytes 2621440

commit v2 on v1

--- a/solution.py
+++ b/solution.py
@@ -13,7 +13,7 @@
 FIRST, EXTRA = 16, 4
 LANES = 128
 BUFS = 8
-PLAN = ((6, 5),)
+PLAN = ((4, 5),)
 
 
 def mm(a, b):
@@ -82,11 +82,11 @@
 
 def kernel(
     plan,
-    x_hbm, expert_ref, slot_ref, gate_ref, wg, wu, wd, sg, su, sd, y_hbm,
-    ring, x_ref, gates, ups, h_ref, z_out, z_in, r_out, r_in, total, gs, us, hs, acc, zk, send_to, take, fold, unfold, y_ref,
-    ring_sem, x_sem, y_sem, z_out_sem, z_in_sem, r_out_sem, r_in_sem,
+    x_hbm, expert_ref, slot_ref, gate_ref, wg, wu, wd, sg, su, sd, y_ref,
+    ring, x_ref, gates, ups, h_ref, out_box, z_in, r_in, total, gs, us, hs, acc, zk, send_to, take, fold, unfold,
+    ring_sem, x_sem, z_out_sem, z_in_sem, r_out_sem, r_in_sem,
 ):
-    members, tokens = z_out.shape[1], x_ref.shape[0]
+    members, tokens = z_in.shape[1], x_ref.shape[0]
     D, F = x_ref.shape[1], h_ref.shape[1]
     chunks, blocks = D // CH, F // CH
     tile_rows = RT * CH
@@ -166,14 +166,20 @@
         for c in range(chunks):
             total[:, at_col(c)] += mm(hs[...], ring[slot, at_col(c), :])
 
-    def pack(z, out, own, c):
-        main = members * FIRST
-        out[c, :, :, pl.ds(0, CH)] = z[:main].reshape(members, FIRST, CH)
-        rest = jnp.concatenate([z[main:, g * LANES:(g + 1) * LANES] for g in range(CH // LANES)], axis=0)
-        rest = mm(fold[...], rest).astype(z.dtype).reshape(members, FIRST, LANES)
-        out[c, :, :, pl.ds(CH, LANES)] = rest
-        own[c, 0, :, pl.ds(0, CH)] = z[:FIRST]
-        own[c, 0, :, pl.ds(CH, LANES)] = rest[0]
+    def pack(z, own, first, n):
+        main, parts = members * FIRST, CH // LANES
+        rest = [
+            jnp.concatenate([z[main:, c * CH + g * LANES:c * CH + (g + 1) * LANES] for g in range(parts)], axis=0)
+            for c in range(n)
+        ]
+        rest = mm(fold[...], jnp.concatenate(rest, axis=1) if n > 1 else rest[0]).astype(z.dtype)
+        for c in range(n):
+            rows = z[:main, c * CH:(c + 1) * CH].reshape(members, FIRST, CH)
+            last = rest[:, c * LANES:(c + 1) * LANES].reshape(members, FIRST, LANES)
+            out_box[first + c, :, :, pl.ds(0, CH)] = rows
+            out_box[first + c, :, :, pl.ds(CH, LANES)] = last
+            own[first + c, 0, :, pl.ds(0, CH)] = rows[0]
+            own[first + c, 0, :, pl.ds(CH, LANES)] = last[0]
 
     def unpack(box, c):
         main, extra = members * FIRST, members * EXTRA
@@ -182,12 +188,14 @@
         for g in range(CH // LANES):
             zk[pl.ds(main, extra), pl.ds(g * LANES, LANES)] = rest[g * extra:(g + 1) * extra]
 
-    far_first = sorted(range(1, members), key=lambda d: (0 if d & 4 else 1, -bin(d & 10).count("1"), d))
-
-    def send(out, box, out_sem, in_sem, c):
-        for d in far_first:
+    far = sorted((d for d in range(1, members) if d & 4), key=lambda d: (-bin(d & 10).count("1"), d))
+    near = sorted((d for d in range(1, members) if not d & 4), key=lambda d: (-bin(d & 10).count("1"), d))
+    order = [d for i in range(max(len(far), len(near))) for d in far[i:i + 1] + near[i:i + 1]]
+
+    def send(box, out_sem, in_sem, c):
+        for d in order:
             pltpu.make_async_remote_copy(
-                src_ref=out.at[c, d], dst_ref=box.at[c, d], send_sem=out_sem.at[c], recv_sem=in_sem.at[c],
+                src_ref=out_box.at[c, d], dst_ref=box.at[c, d], send_sem=out_sem.at[c], recv_sem=in_sem.at[c],
                 device_id=peer(d), device_id_type=MESH,
             ).start()
 
@@ -195,11 +203,12 @@
         others = box.at[c, pl.ds(1, members - 1)]
         pltpu.make_async_copy(others, others, sem.at[c]).wait()
 
-    def routed_up(g_slot, u_slot, b):
+    def routed_up(g_slot, u_slot, b, begin):
         for j in range(RT):
             cols = pl.ds(pl.multiple_of(b * tile_rows + j * CH, CH), CH)
-            gates[:, cols] += mm(zk[...], ring[g_slot, at_col(j), :])
-            ups[:, cols] += mm(zk[...], ring[u_slot, at_col(j), :])
+            for sums, slot in ((gates, g_slot), (ups, u_slot)):
+                part = mm(zk[...], ring[slot, at_col(j), :])
+                sums[:, cols] = part if begin else sums[:, cols] + part
 
     def routed_h(b):
         for j in range(RT):
@@ -215,6 +224,9 @@
             step = [("sg", block, 1), ("su", block, 1), ("sd", block - 1, 1)]
             stages.append(("shared", sched.add(n_shared, step), 0))
             block += n_shared
+        if n_chunks and chunk == 0:
+            stages.append(("begin", sched.add(groups, [("wg", 0, 1), ("wu", 0, 1)]), 0))
+            chunk, n_chunks = 1, n_chunks - 1
         plain = min(n_chunks, chunks - 1 - chunk)
         if plain > 0:
             i0 = chunk * groups
@@ -273,26 +285,14 @@
 
     x_copy.wait()
 
-    def dispatch(c, carry):
-        z = mm(send_to[...], x_ref[:, at_col(c)]).astype(z_out.dtype)
-        pack(z, z_out, z_in, c)
+    pack(mm(send_to[...], x_ref[...]).astype(x_ref.dtype), z_in, 0, chunks)
+    pl.semaphore_wait(barrier, members - 1)
+
+    def ship(c, carry):
+        send(z_in, z_out_sem, z_in_sem, c)
         return carry
 
-    lax.fori_loop(0, chunks, dispatch, 0)
-    pl.semaphore_wait(barrier, members - 1)
-
-    def ship(c, carry):
-        send(z_out, z_in, z_out_sem, z_in_sem, c)
-        return carry
-
     lax.fori_loop(0, chunks, ship, 0)
-
-    def clear(c, carry):
-        gates[:, at_col(c)] = jnp.zeros((slots, CH), jnp.float32)
-        ups[:, at_col(c)] = jnp.zeros((slots, CH), jnp.float32)
-        return carry
-
-    lax.fori_loop(0, blocks, clear, 0)
     total[...] = jnp.zeros_like(total)
 
     def chunk_here(k):
@@ -310,8 +310,8 @@
                 part += acc[...]
             if p < halves - 1:
                 acc[...] = part
-        pack(part.astype(r_out.dtype), r_out, r_in, c)
-        send(r_out, r_in, r_out_sem, r_in_sem, c)
+        pack(part.astype(x_ref.dtype), r_in, c, 1)
+        send(r_in, r_out_sem, r_in_sem, c)
 
     for name, stage, at in stages:
         if name == "first":
@@ -323,6 +323,12 @@
                 shared_h()
                 shared_up(g, u)
                 shared_down(d)
+        elif name == "begin":
+            chunk_here(0)
+
+            def body(turn, stage=stage):
+                g, u = enter(stage, 0, turn)
+                routed_up(g, u, turn, True)
         elif name == "up":
             def body(turn, stage=stage, at=at):
                 @pl.when(turn % groups == 0)
@@ -330,15 +336,18 @@
                     chunk_here(at + turn // groups)
 
                 g, u = enter(stage, 0, turn)
-                routed_up(g, u, turn % groups)
+                routed_up(g, u, turn % groups, False)
         elif name == "last":
             chunk_here(at)
 
             def body(turn, stage=stage):
                 g, u = enter(stage, 0, turn)
                 routed_h(jnp.maximum(turn - 1, 0))
-                routed_up(g, u, turn)
+                routed_up(g, u, turn, False)
         elif name == "down0":
+            for c in range(chunks):
+                all_of(out_box, z_out_sem, c)
+
             def body(turn, stage=stage):
                 down_steps(stage, turn, 0, True)
         elif name == "down":
@@ -354,16 +363,13 @@
     def combine(c, carry):
         all_of(r_in, r_in_sem, c)
         unpack(r_in, c)
-        y_ref[:, at_col(c)] = (mm(take[...], zk[...]) + total[:, at_col(c)]).astype(y_ref.dtype)
-        pltpu.make_async_copy(y_ref.at[:, at_col(c)], y_hbm.at[0, 0, :, at_col(c)], y_sem.at[c]).start()
+        y_ref[0, 0, :, at_col(c)] = (mm(take[...], zk[...]) + total[:, at_col(c)]).astype(y_ref.dtype)
         return carry
 
     lax.fori_loop(0, chunks, combine, 0)
 
     def settle(c, carry):
-        all_of(z_out, z_out_sem, c)
-        all_of(r_out, r_out_sem, c)
-        pltpu.make_async_copy(y_ref.at[:, at_col(c)], y_hbm.at[0, 0, :, at_col(c)], y_sem.at[c]).wait()
+        all_of(out_box, r_out_sem, c)
         return carry
 
     lax.fori_loop(0, chunks, settle, 0)
@@ -383,16 +389,16 @@
         vmem = pl.BlockSpec(memory_space=pltpu.VMEM)
         return pl.pallas_call(
             functools.partial(kernel, plan),
-            out_shape=jax.ShapeDtypeStruct(x.shape, x.dtype),
+            out_shape=pltpu.VMEM(x.shape, x.dtype),
             in_specs=[hbm] + [vmem] * 3 + [hbm] * 6,
-            out_specs=hbm,
+            out_specs=vmem,
             scratch_shapes=[
                 pltpu.VMEM((BUFS, max(D, RT * CH), CH), bf16),
                 pltpu.VMEM((tokens, D), bf16),
                 pltpu.VMEM((slots, F), f32),
                 pltpu.VMEM((slots, F), f32),
                 pltpu.VMEM((slots, F), bf16),
-                box, box, box, box,
+                box, box, box,
                 pltpu.VMEM((tokens, D), f32),
                 pltpu.VMEM((tokens, CH), f32),
                 pltpu.VMEM((tokens, CH), f32),
@@ -403,13 +409,12 @@
                 pltpu.VMEM((tokens, slots), bf16),
                 pltpu.VMEM((members * FIRST, members * FIRST), bf16),
                 pltpu.VMEM((members * FIRST, members * FIRST), bf16),
-                pltpu.VMEM((tokens, D), bf16),
                 pltpu.SemaphoreType.DMA((BUFS,)),
                 pltpu.SemaphoreType.DMA,
-                sems, sems, sems, sems, sems,
+                sems, sems, sems, sems,
             ],
             compiler_params=pltpu.CompilerParams(
-                collective_id=0, has_side_effects=True, vmem_limit_bytes=67_043_328
+                collective_id=0, has_side_effects=True, vmem_limit_bytes=65_536_000
             ),
         )(
             x, expert.reshape(1, tokens), slot.reshape(1, tokens), gate.reshape(1, tokens),

time: 112 us -> 115 us (1.027)
  Pallas kernels: 109 us -> 114 us
  local copies, waits for them, and re-layouts: 2.46 us -> 1.06 us
    pallas_call x1, Pallas kernels: 109 us -> 114 us  [step(): pl.pallas_call(functools.partial(kernel, plan), out_shape=pltpu.VMEM(x.sh...]
    unnamed x1, local copies, waits for them, and re-layouts: 2.46 us -> 1.06 us
where the time goes in v2:
time: 115 us
  Pallas kernels  114 us (99%)
    pallas_call x1, Pallas kernels, step(): pl.pallas_call(functools.partial(kernel, plan), out_shape=pltpu.VMEM(x.sh...  114 us

profile of v2, /device:TPU:0, one launch (start us, length us, event | category | flops | bytes accessed | tf_op | source)
XLA Modules:
  0.0 115.3 jit_solution(607371957900644589)
XLA Ops:
  0.0 114.2 %shard_map.100 = bf16[1,1,256,2560]{3,2,1,0:T(8,128)(2,1)S(1)} custom-call(bf16[1,1,256,2560]{3,2,1,0:T(8,128)(2,1)} %x_hbm.1, s32[1,256]{1,0:T(1,128)} %bitcast.3, s32[1,256]{1,0:T(1,128)} %bitcast.4, f32[1,256]{1,0:T(1,128)} %bitcast.5, bf16[1,2560,8192]{2,1,0:T(8,128)(2,1)} %wg.1, bf16[1,2560,8192]{2,1,0:T(8,128)(2,1)} %wu.1, bf16[1,8192,2560]{2,1,0:T(8,128)(2,1)} %wd.1, ...), custom_call_target="tpu_custom_call" | custom-call | tf_op jit(solution)/shard_map/pallas_call | solution.py:390
  114.2 1.1 copy.12

commit v3 on v2

--- a/solution.py
+++ b/solution.py
@@ -13,7 +13,7 @@
 FIRST, EXTRA = 16, 4
 LANES = 128
 BUFS = 8
-PLAN = ((4, 5),)
+PLAN = ((9, 5),)
 
 
 def mm(a, b):
@@ -190,7 +190,7 @@
 
     far = sorted((d for d in range(1, members) if d & 4), key=lambda d: (-bin(d & 10).count("1"), d))
     near = sorted((d for d in range(1, members) if not d & 4), key=lambda d: (-bin(d & 10).count("1"), d))
-    order = [d for i in range(max(len(far), len(near))) for d in far[i:i + 1] + near[i:i + 1]]
+    order = far + near
 
     def send(box, out_sem, in_sem, c):
         for d in order:

time: 115 us -> 109 us (0.948)
  Pallas kernels: 114 us -> 108 us
    pallas_call x1, Pallas kernels: 114 us -> 108 us  [step(): pl.pallas_call(functools.partial(kernel, plan), out_shape=pltpu.VMEM(x.sh...]
where the time goes in v3:
time: 109 us
  Pallas kernels  108 us (99%)
    pallas_call x1, Pallas kernels, step(): pl.pallas_call(functools.partial(kernel, plan), out_shape=pltpu.VMEM(x.sh...  108 us

profile of v3, /device:TPU:0, one launch (start us, length us, event | category | flops | bytes accessed | tf_op | source)
XLA Modules:
  0.0 109.1 jit_solution(10587587270033845907)
XLA Ops:
  0.0 108.1 %shard_map.100 = bf16[1,1,256,2560]{3,2,1,0:T(8,128)(2,1)S(1)} custom-call(bf16[1,1,256,2560]{3,2,1,0:T(8,128)(2,1)} %x_hbm.1, s32[1,256]{1,0:T(1,128)} %bitcast.3, s32[1,256]{1,0:T(1,128)} %bitcast.4, f32[1,256]{1,0:T(1,128)} %bitcast.5, bf16[1,2560,8192]{2,1,0:T(8,128)(2,1)} %wg.1, bf16[1,2560,8192]{2,1,0:T(8,128)(2,1)} %wu.1, bf16[1,8192,2560]{2,1,0:T(8,128)(2,1)} %wd.1, ...), custom_call_target="tpu_custom_call" | custom-call | tf_op jit(solution)/shard_map/pallas_call | solution.py:390
  108.1 1.1 copy.12
